TPU v7x, 32 devices: a whole 2x2x4 slice. The times are simulated.
32 devices in a mesh: pipe: 2 (over x), tensor: 4 (over y, core), expert: 4 (over z).
Axes of the slice: x: 2, y: 2, z: 4, core: 2. Of those that a mesh axis runs over, the one named last changes fastest.
Arguments:
- tokens: bfloat16 [2, 256, 4096], P(None, 'expert'), may hold values from -6 to 6
- gains: float32 [2, 4096], P('pipe'), may hold values from 0.1 to 1.9
- route_ids: int32 [2, 2, 256, 2], P('pipe', None, 'expert'), may hold values from 0 to 3, all different within a row
- route_weights: float32 [2, 2, 256, 2], P('pipe', None, 'expert'), may hold values from 0.2 to 1
- picks: int32 [2, 2, 4, 64], P('pipe', None, 'expert'), may hold values from 0 to 63, each once within a row
- w_gate: bfloat16 [2, 4, 4096, 1536], P('pipe', 'expert', None, 'tensor'), may hold values from -0.09375 to 0.09375
- w_up: bfloat16 [2, 4, 4096, 1536], P('pipe', 'expert', None, 'tensor'), may hold values from -0.09375 to 0.09375
- w_down: bfloat16 [2, 4, 1536, 4096], P('pipe', 'expert', 'tensor'), may hold values from -0.15625 to 0.15625
Outputs:
- streams: bfloat16 [2, 2, 256, 4096], P('pipe', None, 'expert', 'tensor')
Inputs may be any that keep to these rules, and one draw needn't show every extreme that they name: `route_ids`: each token names 2 different experts; every expert is named by some token. `picks`: for every layer, micro-batch and block of 64 tokens, a permutation of 0 to 63.
All inputs are finite; a program needn't handle non-finite values.
Results may differ from a plain program's by a relative error of at most 0.025.
Values may be sent and summed in bfloat16 or wider, within the bound.
A program may use at most 64 MiB of HBM per device.

v0:
```python
import functools

import jax
import jax.numpy as jnp
from jax import lax
from jax.experimental import pallas as pl
from jax.experimental.pallas import tpu as pltpu
from jax.sharding import PartitionSpec as P

epsilon = 1e-06
MESH = pl.DeviceIdType.MESH
F32 = jnp.float32
BF16 = jnp.bfloat16


def layer_kernel(
    sizes, tokens, gains, placing, comb, w_gate, w_up, w_down, out,
    h_in, fresh, send, x, wg, wu, wd, g_acc, u_acc, own, p_send, p_recv,
    y_send, y_recv, z_send, ret,
    w_sem, h_loc, h_send, h_recv, d_send, d_recv, f_send, f_recv, c_send, c_recv,
    ps_sem, pr_sem, ys_sem, yr_sem, zs_sem, zr_sem,
):
    micros, n_p, n_t, n_e, pair, rows_ge, width = sizes
    n_a = n_t // pair
    cut = (n_e + 1) // 2
    halves = [list(range(cut)), list(range(cut, n_e))]
    p = lax.axis_index("pipe")
    r = lax.axis_index("tensor")
    z = lax.axis_index("expert")
    a = lax.div(r, pair)
    c = lax.rem(r, pair)

    def peer_e(d):
        return lax.rem(z + d, n_e)

    def rank_of(da, dc):
        return lax.rem(a + da, n_a) * pair + lax.rem(c + dc, pair)

    def remote(src, dst, ssem, rsem, where):
        return pltpu.make_async_remote_copy(
            src_ref=src, dst_ref=dst, send_sem=ssem, recv_sem=rsem,
            device_id=where, device_id_type=MESH,
        )

    loads = [
        pltpu.make_async_copy(w_gate.at[0, 0], wg, w_sem.at[0]),
        pltpu.make_async_copy(w_up.at[0, 0], wu, w_sem.at[1]),
        pltpu.make_async_copy(w_down.at[0, 0], wd, w_sem.at[2]),
    ]

    def first_load(m):
        cols = pl.ds(pl.multiple_of(r * width, width), width)
        return pltpu.make_async_copy(tokens.at[m, :, cols], h_in.at[m], h_loc.at[m])

    @pl.when(p == 0)
    def _():
        for m in range(micros):
            first_load(m).start()

    for load in loads:
        load.start()

    barrier = pltpu.get_barrier_semaphore()

    def greet(where):
        pl.semaphore_signal(barrier, inc=1, device_id=where, device_id_type=MESH)

    for d in range(1, n_e):
        greet({"expert": peer_e(d)})
    for da in range(1, n_a):
        greet({"tensor": rank_of(da, 0)})
    for dc in range(1, pair):
        greet({"tensor": rank_of(0, dc)})

    @pl.when(p > 0)
    def _():
        greet({"pipe": p - 1})

    @pl.when(p < n_p - 1)
    def _():
        greet({"pipe": p + 1})

    ends = jnp.where(p > 0, 1, 0) + jnp.where(p < n_p - 1, 1, 0)
    pl.semaphore_wait(barrier, n_e - 1 + n_a - 1 + pair - 1 + ends)

    def relay(m):
        return remote(fresh.at[m], h_in.at[m], h_send.at[m], h_recv.at[m],
                      {"pipe": jnp.minimum(p + 1, n_p - 1)})

    def d_copy(m, d):
        return remote(send.at[m, d], x.at[m, r, z], d_send.at[m, d], d_recv.at[m, d],
                      {"expert": peer_e(d)})

    def f_copy(m, d, da):
        block = x.at[m, r, peer_e(n_e - d)]
        return remote(block, block, f_send.at[m, d, da], f_recv.at[m, d, da],
                      {"tensor": rank_of(da, 0)})

    def c_copy(m, d, da):
        block = x.at[m, rank_of(da, 0), peer_e(n_e - d)]
        return remote(block, block, c_send.at[m, d, da], c_recv.at[m, d, da],
                      {"tensor": rank_of(0, 1)})

    def p_copy(m, h, da):
        return remote(p_send.at[m, h, da], p_recv.at[m, h, da], ps_sem.at[m, h, da],
                      pr_sem.at[m, h, da], {"tensor": rank_of(0, 1)})

    def y_copy(m, d, da):
        return remote(y_send.at[m, d, da], y_recv.at[m, d, da], ys_sem.at[m, d, da],
                      yr_sem.at[m, d, da], {"tensor": rank_of(da, 0)})

    def z_copy(m, d):
        return remote(z_send.at[m, d], ret.at[m, z], zs_sem.at[m, d], zr_sem.at[m, d],
                      {"expert": peer_e(n_e - d)})

    def dispatch(m):
        @pl.when(p == 0)
        def _():
            first_load(m).wait()

        @pl.when(p > 0)
        def _():
            relay(m).wait_recv()

        h = h_in[m]
        for d in list(range(1, n_e)) + [0]:
            block = jnp.dot(placing[m, peer_e(d)], h, preferred_element_type=F32).astype(BF16)
            if d:
                send[m, d] = block
                d_copy(m, d).start()
            else:
                x[m, r, z] = block

    def forward(m, d):
        if d:
            d_copy(m, d).wait_recv()
        for da in range(1, n_a):
            f_copy(m, d, da).start()
        if pair > 1:
            c_copy(m, d, 0).start()

    def pass_on(m, d):
        for da in range(1, n_a):
            f_copy(m, d, da).wait_recv()
            if pair > 1:
                c_copy(m, d, da).start()

    def compute(m, h):
        if m == 0 and h == 0:
            for load in loads:
                load.wait()
        if pair > 1:
            for d in halves[h]:
                for da in range(n_a):
                    c_copy(m, d, da).wait_recv()
        homes = [peer_e(n_e - d) for d in halves[h]]

        def rows_of(q):
            return jnp.concatenate([x[m, q, g].astype(F32) for g in homes], axis=0)

        ss = jnp.zeros((len(homes) * rows_ge, 1), F32)
        for q in range(n_t):
            xf = rows_of(q)
            ss = ss + jnp.sum(xf * xf, axis=-1, keepdims=True)
        inv = lax.rsqrt(ss * (1.0 / (n_t * width)) + epsilon)
        for q in range(n_t):
            cols = slice(q * width, (q + 1) * width)
            nq = (rows_of(q) * inv * gains[0:1, cols]).astype(BF16)
            gq = jnp.dot(nq, wg[cols, :], preferred_element_type=F32)
            uq = jnp.dot(nq, wu[cols, :], preferred_element_type=F32)
            if q == 0:
                g_acc[...] = gq
                u_acc[...] = uq
            else:
                g_acc[...] += gq
                u_acc[...] += uq
        gate = g_acc[...]
        hidden = (gate / (1.0 + jnp.exp(-gate)) * u_acc[...]).astype(BF16)
        for dc in list(range(1, pair)) + [0]:
            for da in list(range(1, n_a)) + [0]:
                start = pl.multiple_of(rank_of(da, dc) * width, width)
                part = jnp.dot(hidden, wd[:, pl.ds(start, width)], preferred_element_type=F32)
                if dc:
                    p_send[m, h, da] = part.astype(BF16)
                    p_copy(m, h, da).start()
                else:
                    own[m, h, da] = part.astype(BF16)

    def reduce_pair(m, h):
        for da in list(range(1, n_a)) + [0]:
            if pair > 1:
                p_copy(m, h, da).wait_recv()
            for i, d in enumerate(halves[h]):
                part = slice(i * rows_ge, (i + 1) * rows_ge)
                total = own[m, h, da, part].astype(F32)
                if pair > 1:
                    total = total + p_recv[m, h, da, part].astype(F32)
                y_send[m, d, da] = total.astype(BF16)
                if da:
                    y_copy(m, d, da).start()

    def reduce_far(m, d):
        total = y_send[m, d, 0].astype(F32)
        for da in range(1, n_a):
            y_copy(m, d, da).wait_recv()
            total = total + y_recv[m, d, da].astype(F32)
        if d:
            z_send[m, d] = total.astype(BF16)
            z_copy(m, d).start()
        else:
            ret[m, z] = total.astype(BF16)

    def combine(m):
        toks = h_in.shape[1]
        for d in range(n_e):
            e = peer_e(d)
            if d:
                z_copy(m, d).wait_recv()
            both = jnp.dot(comb[m, e], ret[m, e], preferred_element_type=F32)
            g_part = both[:toks] + both[toks:]
            update = g_part if d == 0 else update + g_part
        new = (h_in[m].astype(F32) + update).astype(BF16)
        fresh[m] = new
        out[0, m] = new

        @pl.when(p < n_p - 1)
        def _():
            relay(m).start()

    near, far = halves[0], halves[-1]

    def step(fn, *args):
        return functools.partial(fn, *args)

    def head(m):
        steps = [step(forward, m, d) for d in near]
        steps += [step(pass_on, m, d) for d in near[:-1]]
        steps += [step(forward, m, far[0]), step(pass_on, m, near[-1])]
        return steps

    def middle(m):
        steps = [step(compute, m, 0)]
        steps += [step(forward, m, d) for d in far[1:]]
        steps += [step(pass_on, m, d) for d in far[:-1]]
        steps += [step(reduce_pair, m, 0), step(pass_on, m, far[-1])]
        return steps

    def back(m):
        return [step(compute, m, 1), step(reduce_pair, m, 1)]

    def tail(m):
        return [step(reduce_far, m, d) for d in near[1:] + near[:1] + far]

    def both_of(one, two):
        mixed = []
        for i in range(max(len(one), len(two))):
            mixed += one[i:i + 1] + two[i:i + 1]
        return mixed

    dispatch(0)

    @pl.when(p == 0)
    def _():
        for m in range(1, micros):
            dispatch(m)

    def late_dispatch(m):
        @pl.when(p > 0)
        def _():
            dispatch(m)

    plan = head(0)
    for m in range(micros):
        plan += middle(m)
        if m:
            plan += [step(combine, m - 1)]
        plan += back(m)
        if m + 1 < micros:
            plan += [step(late_dispatch, m + 1)]
            plan += both_of(tail(m), head(m + 1))
    plan += tail(micros - 1) + [step(combine, micros - 1)]
    for go in plan:
        go()

    for m in range(micros):
        for d in range(n_e):
            if d:
                d_copy(m, d).wait_send()
                z_copy(m, d).wait_send()
            for da in range(n_a):
                if da:
                    f_copy(m, d, da).wait_send()
                    y_copy(m, d, da).wait_send()
                if pair > 1:
                    c_copy(m, d, da).wait_send()
        if pair > 1:
            for h in range(len(halves)):
                for da in range(n_a):
                    p_copy(m, h, da).wait_send()

        @pl.when(p < n_p - 1)
        def _():
            relay(m).wait_send()


def local(mesh_shape, tokens, gains, route_ids, route_weights, picks, w_gate, w_up, w_down):
    n_p, n_t, n_e = mesh_shape
    micros, toks, model_width = tokens.shape
    route_count = route_ids.shape[3]
    quarter = toks // n_t
    capacity = 4 * quarter * route_count // (3 * n_e)
    width = model_width // n_t
    pair = 2 if n_t % 2 == 0 else 1
    n_a = n_t // pair
    rows_ge = -(-n_t * capacity // 8) * 8
    cut = (n_e + 1) // 2
    rows = cut * rows_ge
    hidden_width = w_gate.shape[3]

    ids = route_ids[0]
    weights = route_weights[0]
    order = picks[0, :, 0]
    each = jnp.arange(toks, dtype=jnp.int32)
    experts = jnp.arange(n_e, dtype=jnp.int32)
    hit = order[:, None, :] == each[None, :, None]
    pos = jnp.sum(jnp.where(hit, each[None, None, :], 0), axis=2)
    block = pos // quarter
    named = ids[:, :, :, None] == experts
    names = jnp.any(named, axis=2)
    w_te = jnp.sum(jnp.where(named, weights[..., None], 0.0), axis=2)
    before = (block[:, :, None] == block[:, None, :]) & (pos[:, None, :] < pos[:, :, None])
    slot = jnp.sum((before[..., None] & names[:, None]).astype(jnp.int32), axis=2)
    target = jnp.where(names & (slot < capacity), block[..., None] * capacity + slot, -1)
    target = target.transpose(0, 2, 1)
    w_et = w_te.transpose(0, 2, 1)
    places = jnp.arange(rows_ge, dtype=jnp.int32)
    placing = (places[None, None, :, None] == target[:, :, None, :]).astype(BF16)
    spread = target[..., None] == places
    high = lax.reduce_precision(w_et, 8, 7)
    low = w_et - high
    comb = jnp.concatenate(
        [jnp.where(spread, high[..., None], 0.0), jnp.where(spread, low[..., None], 0.0)], axis=2
    ).astype(BF16)

    sizes = (micros, n_p, n_t, n_e, pair, rows_ge, width)
    dma = pltpu.SemaphoreType.DMA
    vmem = pl.BlockSpec(memory_space=pltpu.VMEM)
    anywhere = pl.BlockSpec(memory_space=pl.ANY)
    return pl.pallas_call(
        functools.partial(layer_kernel, sizes),
        out_shape=jax.ShapeDtypeStruct((1, micros, toks, width), BF16),
        in_specs=[anywhere, vmem, vmem, vmem, anywhere, anywhere, anywhere],
        out_specs=vmem,
        scratch_shapes=[
            pltpu.VMEM((micros, toks, width), BF16),
            pltpu.VMEM((micros, toks, width), BF16),
            pltpu.VMEM((micros, n_e, rows_ge, width), BF16),
            pltpu.VMEM((micros, n_t, n_e, rows_ge, width), BF16),
            pltpu.VMEM(w_gate.shape[2:], BF16),
            pltpu.VMEM(w_up.shape[2:], BF16),
            pltpu.VMEM(w_down.shape[2:], BF16),
            pltpu.VMEM((rows, hidden_width), F32),
            pltpu.VMEM((rows, hidden_width), F32),
            pltpu.VMEM((micros, 2, n_a, rows, width), BF16),
            pltpu.VMEM((micros, 2, n_a, rows, width), BF16),
            pltpu.VMEM((micros, 2, n_a, rows, width), BF16),
            pltpu.VMEM((micros, n_e, n_a, rows_ge, width), BF16),
            pltpu.VMEM((micros, n_e, n_a, rows_ge, width), BF16),
            pltpu.VMEM((micros, n_e, rows_ge, width), BF16),
            pltpu.VMEM((micros, n_e, rows_ge, width), BF16),
            dma((3,)), dma((micros,)), dma((micros,)), dma((micros,)),
            dma((micros, n_e)), dma((micros, n_e)),
            dma((micros, n_e, n_a)), dma((micros, n_e, n_a)),
            dma((micros, n_e, n_a)), dma((micros, n_e, n_a)),
            dma((micros, 2, n_a)), dma((micros, 2, n_a)),
            dma((micros, n_e, n_a)), dma((micros, n_e, n_a)),
            dma((micros, n_e)), dma((micros, n_e)),
        ],
        compiler_params=pltpu.CompilerParams(
            collective_id=0, has_side_effects=True, vmem_limit_bytes=67043328
        ),
    )(tokens, gains, placing, comb, w_gate, w_up, w_down)


def solution(mesh):
    mesh_shape = (mesh.shape["pipe"], mesh.shape["tensor"], mesh.shape["expert"])
    return jax.shard_map(
        functools.partial(local, mesh_shape),
        mesh=mesh,
        in_specs=(
            P(None, "expert", None),
            P("pipe", None),
            P("pipe", None, "expert", None),
            P("pipe", None, "expert", None),
            P("pipe", None, "expert", None),
            P("pipe", "expert", None, "tensor"),
            P("pipe", "expert", None, "tensor"),
            P("pipe", "expert", "tensor", None),
        ),
        out_specs=P("pipe", None, "expert", "tensor"),
        check_vma=False,
    )
```

profile of v0, /device:TPU:2, one launch (start us, length us, event | category | flops | bytes accessed | tf_op | source)
XLA Modules:
  0.0 106.7 jit_solution(5242791070049398086)
XLA Ops:
  0.0 0.7 fusion.1
  0.7 0.8 select_reduce_fusion
  1.5 0.7 select_reduce_fusion.1
  2.2 0.1 compare_and_fusion
  2.3 0.2 convert_reduce_fusion
  2.6 0.7 fusion.placing
  3.3 0.1 pad_maximum_fusion
  3.4 0.9 copy.16.comb
  4.2 100.8 %shard_map.82 = bf16[1,2,64,1024]{3,2,1,0:T(8,128)(2,1)} custom-call(bf16[2,64,4096]{2,1,0:T(8,128)(2,1)} %tokens.1, f32[1,4096]{1,0:T(1,128)} %gains.1, bf16[2,4,40,64]{3,2,1,0:T(8,128)(2,1)} %fusion.placing, bf16[2,4,128,40]{3,2,1,0:T(8,128)(2,1)} %copy.16.comb, bf16[1,1,4096,384]{3,2,1,0:T(8,128)(2,1)} %w_gate.1, bf16[1,1,4096,384]{3,2,1,0:T(8,128)(2,1)} %w_up.1, ...), custom_call_target="tpu_custom_call" | custom-call | tf_op jit(solution)/shard_map/pallas_call | solution.py:349
  105.0 1.7 %copy.18 = bf16[1,2,64,1024]{3,2,1,0:T(8,128)(2,1)} copy(bf16[1,2,64,1024]{3,2,1,0:T(8,128)(2,1)} %shard_map.82) | data formatting | bytes 524288
  (4 shorter events, 0.1 us)
where the time goes:
time: 107 us
  Pallas kernels  101 us (94%)
  other arithmetic  3.33 us (3%)
  local copies, waits for them, and re-layouts  2.52 us (2%)
    pallas_call x1, Pallas kernels, local(): pl.pallas_call(functools.partial(layer_kernel, sizes), out_shape=jax.Shap...  101 us

commit v1 on v0

--- a/solution.py
+++ b/solution.py
@@ -14,16 +14,16 @@
 
 
 def layer_kernel(
-    sizes, tokens, gains, placing, comb, w_gate, w_up, w_down, out,
-    h_in, fresh, send, x, wg, wu, wd, g_acc, u_acc, own, p_send, p_recv,
+    sizes, tokens, gains, ids, weights, picks, w_gate, w_up, w_down, out,
+    placing, comb, h_in, fresh, send, x, wg, wu, wd, g_acc, u_acc, own, p_send, p_recv,
     y_send, y_recv, z_send, ret,
     w_sem, h_loc, h_send, h_recv, d_send, d_recv, f_send, f_recv, c_send, c_recv,
     ps_sem, pr_sem, ys_sem, yr_sem, zs_sem, zr_sem,
 ):
-    micros, n_p, n_t, n_e, pair, rows_ge, width = sizes
+    micros, n_p, n_t, n_e, pair, rows_ge, width, capacity = sizes
     n_a = n_t // pair
     cut = (n_e + 1) // 2
-    halves = [list(range(cut)), list(range(cut, n_e))]
+    halves = [list(range(n_e - 1, cut - 1, -1)), list(range(cut - 1, -1, -1))]
     p = lax.axis_index("pipe")
     r = lax.axis_index("tensor")
     z = lax.axis_index("expert")
@@ -80,6 +80,49 @@
     def _():
         greet({"pipe": p + 1})
 
+    toks = h_in.shape[1]
+    quarter = toks // n_t
+    down = lax.broadcasted_iota(jnp.int32, (toks, toks), 0)
+    across = lax.broadcasted_iota(jnp.int32, (toks, toks), 1)
+    same = down == across
+
+    def column(row):
+        return jnp.sum(jnp.where(same, row, jnp.zeros_like(row)), axis=1, keepdims=True)
+
+    def row_of(col):
+        return jnp.sum(jnp.where(same, col, jnp.zeros_like(col)), axis=0, keepdims=True)
+
+    def slots(m):
+        pos = jnp.sum(jnp.where(picks[m] == down, across, 0), axis=1, keepdims=True)
+        pos_row = row_of(pos)
+        block = lax.div(pos, quarter)
+        before = (lax.div(pos_row, quarter) == block) & (pos_row < pos)
+        found = []
+        for e in range(n_e):
+            named = jnp.zeros((1, toks), jnp.int32)
+            for k in range(ids.shape[1]):
+                named = named + jnp.where(ids[m, k:k + 1] == e, 1, 0)
+            slot = jnp.sum(jnp.where(before, named, 0), axis=1, keepdims=True)
+            kept = (column(named) > 0) & (slot < capacity)
+            found.append(jnp.where(kept, block * capacity + slot, -1))
+        return found
+
+    def place(m):
+        places = lax.broadcasted_iota(jnp.int32, (rows_ge, toks), 0)
+        for e, target in enumerate(slots(m)):
+            placing[m, e] = jnp.where(places == row_of(target), 1.0, 0.0).astype(BF16)
+            w_row = jnp.zeros((1, toks), F32)
+            for k in range(ids.shape[1]):
+                w_row = w_row + jnp.where(ids[m, k:k + 1] == e, weights[m, k:k + 1], 0.0)
+            spread = lax.broadcasted_iota(jnp.int32, (toks, rows_ge), 1) == target
+            w_col = jnp.where(spread, column(w_row), 0.0)
+            high = w_col.astype(BF16)
+            comb[m, e, :toks] = high
+            comb[m, e, toks:] = (w_col - high.astype(F32)).astype(BF16)
+
+    for m in range(micros):
+        place(m)
+
     ends = jnp.where(p > 0, 1, 0) + jnp.where(p < n_p - 1, 1, 0)
     pl.semaphore_wait(barrier, n_e - 1 + n_a - 1 + pair - 1 + ends)
 
@@ -123,7 +166,7 @@
             relay(m).wait_recv()
 
         h = h_in[m]
-        for d in list(range(1, n_e)) + [0]:
+        for d in range(n_e - 1, -1, -1):
             block = jnp.dot(placing[m, peer_e(d)], h, preferred_element_type=F32).astype(BF16)
             if d:
                 send[m, d] = block
@@ -211,7 +254,6 @@
             ret[m, z] = total.astype(BF16)
 
     def combine(m):
-        toks = h_in.shape[1]
         for d in range(n_e):
             e = peer_e(d)
             if d:
@@ -227,29 +269,29 @@
         def _():
             relay(m).start()
 
-    near, far = halves[0], halves[-1]
+    first, second = halves
 
     def step(fn, *args):
         return functools.partial(fn, *args)
 
     def head(m):
-        steps = [step(forward, m, d) for d in near]
-        steps += [step(pass_on, m, d) for d in near[:-1]]
-        steps += [step(forward, m, far[0]), step(pass_on, m, near[-1])]
+        steps = [step(forward, m, 0), step(forward, m, first[0]), step(pass_on, m, 0)]
+        steps += [step(forward, m, d) for d in first[1:]]
+        steps += [step(pass_on, m, d) for d in first]
         return steps
 
     def middle(m):
         steps = [step(compute, m, 0)]
-        steps += [step(forward, m, d) for d in far[1:]]
-        steps += [step(pass_on, m, d) for d in far[:-1]]
-        steps += [step(reduce_pair, m, 0), step(pass_on, m, far[-1])]
+        steps += [step(forward, m, d) for d in second[:-1]]
+        steps += [step(reduce_pair, m, 0)]
+        steps += [step(pass_on, m, d) for d in second[:-1]]
         return steps
 
     def back(m):
         return [step(compute, m, 1), step(reduce_pair, m, 1)]
 
     def tail(m):
-        return [step(reduce_far, m, d) for d in near[1:] + near[:1] + far]
+        return [step(reduce_far, m, d) for d in first + second]
 
     def both_of(one, two):
         mixed = []
@@ -317,41 +359,22 @@
     rows = cut * rows_ge
     hidden_width = w_gate.shape[3]
 
-    ids = route_ids[0]
-    weights = route_weights[0]
-    order = picks[0, :, 0]
-    each = jnp.arange(toks, dtype=jnp.int32)
-    experts = jnp.arange(n_e, dtype=jnp.int32)
-    hit = order[:, None, :] == each[None, :, None]
-    pos = jnp.sum(jnp.where(hit, each[None, None, :], 0), axis=2)
-    block = pos // quarter
-    named = ids[:, :, :, None] == experts
-    names = jnp.any(named, axis=2)
-    w_te = jnp.sum(jnp.where(named, weights[..., None], 0.0), axis=2)
-    before = (block[:, :, None] == block[:, None, :]) & (pos[:, None, :] < pos[:, :, None])
-    slot = jnp.sum((before[..., None] & names[:, None]).astype(jnp.int32), axis=2)
-    target = jnp.where(names & (slot < capacity), block[..., None] * capacity + slot, -1)
-    target = target.transpose(0, 2, 1)
-    w_et = w_te.transpose(0, 2, 1)
-    places = jnp.arange(rows_ge, dtype=jnp.int32)
-    placing = (places[None, None, :, None] == target[:, :, None, :]).astype(BF16)
-    spread = target[..., None] == places
-    high = lax.reduce_precision(w_et, 8, 7)
-    low = w_et - high
-    comb = jnp.concatenate(
-        [jnp.where(spread, high[..., None], 0.0), jnp.where(spread, low[..., None], 0.0)], axis=2
-    ).astype(BF16)
-
-    sizes = (micros, n_p, n_t, n_e, pair, rows_ge, width)
+    ids = route_ids[0].transpose(0, 2, 1)
+    weights = route_weights[0].transpose(0, 2, 1)
+    order = picks[0]
+
+    sizes = (micros, n_p, n_t, n_e, pair, rows_ge, width, capacity)
     dma = pltpu.SemaphoreType.DMA
     vmem = pl.BlockSpec(memory_space=pltpu.VMEM)
     anywhere = pl.BlockSpec(memory_space=pl.ANY)
     return pl.pallas_call(
         functools.partial(layer_kernel, sizes),
         out_shape=jax.ShapeDtypeStruct((1, micros, toks, width), BF16),
-        in_specs=[anywhere, vmem, vmem, vmem, anywhere, anywhere, anywhere],
+        in_specs=[anywhere, vmem, vmem, vmem, vmem, anywhere, anywhere, anywhere],
         out_specs=vmem,
         scratch_shapes=[
+            pltpu.VMEM((micros, n_e, rows_ge, toks), BF16),
+            pltpu.VMEM((micros, n_e, 2 * toks, rows_ge), BF16),
             pltpu.VMEM((micros, toks, width), BF16),
             pltpu.VMEM((micros, toks, width), BF16),
             pltpu.VMEM((micros, n_e, rows_ge, width), BF16),
@@ -377,9 +400,9 @@
             dma((micros, n_e)), dma((micros, n_e)),
         ],
         compiler_params=pltpu.CompilerParams(
-            collective_id=0, has_side_effects=True, vmem_limit_bytes=67043328
+            collective_id=0, has_side_effects=True, vmem_limit_bytes=67043328 - 600 * 1024
         ),
-    )(tokens, gains, placing, comb, w_gate, w_up, w_down)
+    )(tokens, gains, ids, weights, order, w_gate, w_up, w_down)
 
 
 def solution(mesh):

time: 107 us -> 111 us (1.037)
  Pallas kernels: 101 us -> 108 us
  other arithmetic: 3.33 us -> 0 us
    pallas_call x1, Pallas kernels: 101 us -> 108 us  [local(): pl.pallas_call(functools.partial(layer_kernel, sizes), out_shape=jax.Shap...]
    reduce_sum x3 -> x0, other arithmetic: 1.73 us -> none  [the longest x1 0.79 us: local(): pos = jnp.sum(jnp.where(hit, each[None, None, :], 0), axis=2)]
where the time goes in v1:
time: 111 us; the launch traced here: 110 us
  Pallas kernels  108 us (97%)
  local copies, waits for them, and re-layouts  1.67 us (2%)
    pallas_call x1, Pallas kernels, local(): pl.pallas_call(functools.partial(layer_kernel, sizes), out_shape=jax.Shap...  108 us

profile of v1, /device:TPU:2, one launch (start us, length us, event | category | flops | bytes accessed | tf_op | source)
XLA Modules:
  0.0 109.8 jit_solution(5014242967065071961)
XLA Ops:
  0.0 108.2 %shard_map.82 = bf16[1,2,64,1024]{3,2,1,0:T(8,128)(2,1)} custom-call(bf16[2,64,4096]{2,1,0:T(8,128)(2,1)} %tokens.1, f32[1,4096]{1,0:T(1,128)} %gains.1, s32[2,2,64]{2,1,0:T(2,128)} %bitcast.9, f32[2,2,64]{2,1,0:T(2,128)} %bitcast.10, s32[2,1,64]{2,1,0:T(1,128)} %bitcast.11, bf16[1,1,4096,384]{3,2,1,0:T(8,128)(2,1)} %w_gate.1, ...), custom_call_target="tpu_custom_call" | custom-call | tf_op jit(solution)/shard_map/pallas_call | solution.py:370
  108.2 1.7 %copy.11 = bf16[1,2,64,1024]{3,2,1,0:T(8,128)(2,1)} copy(bf16[1,2,64,1024]{3,2,1,0:T(8,128)(2,1)} %shard_map.82) | data formatting | bytes 524288

commit v2 on v1

--- a/solution.py
+++ b/solution.py
@@ -23,7 +23,7 @@
     micros, n_p, n_t, n_e, pair, rows_ge, width, capacity = sizes
     n_a = n_t // pair
     cut = (n_e + 1) // 2
-    halves = [list(range(n_e - 1, cut - 1, -1)), list(range(cut - 1, -1, -1))]
+    halves = [list(range(cut)), list(range(n_e - 1, cut - 1, -1))]
     p = lax.axis_index("pipe")
     r = lax.axis_index("tensor")
     z = lax.axis_index("expert")
@@ -31,7 +31,12 @@
     c = lax.rem(r, pair)
 
     def peer_e(d):
-        return lax.rem(z + d, n_e)
+        other = z
+        for bit in range(n_e.bit_length()):
+            one = 1 << bit
+            if d & one:
+                other = other + one * (1 - 2 * lax.rem(lax.div(z, one), 2))
+        return other
 
     def rank_of(da, dc):
         return lax.rem(a + da, n_a) * pair + lax.rem(c + dc, pair)
@@ -135,12 +140,12 @@
                       {"expert": peer_e(d)})
 
     def f_copy(m, d, da):
-        block = x.at[m, r, peer_e(n_e - d)]
+        block = x.at[m, r, peer_e(d)]
         return remote(block, block, f_send.at[m, d, da], f_recv.at[m, d, da],
                       {"tensor": rank_of(da, 0)})
 
     def c_copy(m, d, da):
-        block = x.at[m, rank_of(da, 0), peer_e(n_e - d)]
+        block = x.at[m, rank_of(da, 0), peer_e(d)]
         return remote(block, block, c_send.at[m, d, da], c_recv.at[m, d, da],
                       {"tensor": rank_of(0, 1)})
 
@@ -154,7 +159,7 @@
 
     def z_copy(m, d):
         return remote(z_send.at[m, d], ret.at[m, z], zs_sem.at[m, d], zr_sem.at[m, d],
-                      {"expert": peer_e(n_e - d)})
+                      {"expert": peer_e(d)})
 
     def dispatch(m):
         @pl.when(p == 0)
@@ -166,7 +171,7 @@
             relay(m).wait_recv()
 
         h = h_in[m]
-        for d in range(n_e - 1, -1, -1):
+        for d in halves[0][1:] + halves[1] + [0]:
             block = jnp.dot(placing[m, peer_e(d)], h, preferred_element_type=F32).astype(BF16)
             if d:
                 send[m, d] = block
@@ -196,7 +201,7 @@
             for d in halves[h]:
                 for da in range(n_a):
                     c_copy(m, d, da).wait_recv()
-        homes = [peer_e(n_e - d) for d in halves[h]]
+        homes = [peer_e(d) for d in halves[h]]
 
         def rows_of(q):
             return jnp.concatenate([x[m, q, g].astype(F32) for g in homes], axis=0)
@@ -274,24 +279,32 @@
     def step(fn, *args):
         return functools.partial(fn, *args)
 
+    def when(test, fn, *args):
+        pl.when(test)(functools.partial(fn, *args))
+
     def head(m):
-        steps = [step(forward, m, 0), step(forward, m, first[0]), step(pass_on, m, 0)]
-        steps += [step(forward, m, d) for d in first[1:]]
-        steps += [step(pass_on, m, d) for d in first]
+        steps = [step(forward, m, d) for d in first]
+        steps += [step(pass_on, m, d) for d in first[:-1]]
+        steps += [step(forward, m, second[0]), step(pass_on, m, first[-1])]
+        if m:
+            steps += [step(when, p == 0, forward, m, d) for d in second[1:]]
         return steps
 
     def middle(m):
         steps = [step(compute, m, 0)]
-        steps += [step(forward, m, d) for d in second[:-1]]
-        steps += [step(reduce_pair, m, 0)]
+        if m:
+            steps += [step(when, p > 0, forward, m, d) for d in second[1:]]
+        else:
+            steps += [step(forward, m, d) for d in second[1:]]
         steps += [step(pass_on, m, d) for d in second[:-1]]
+        steps += [step(reduce_pair, m, 0), step(pass_on, m, second[-1])]
         return steps
 
     def back(m):
         return [step(compute, m, 1), step(reduce_pair, m, 1)]
 
     def tail(m):
-        return [step(reduce_far, m, d) for d in first + second]
+        return [step(reduce_far, m, d) for d in first[1:] + first[:1] + second]
 
     def both_of(one, two):
         mixed = []
@@ -315,12 +328,14 @@
     for m in range(micros):
         plan += middle(m)
         if m:
-            plan += [step(combine, m - 1)]
+            plan += [step(when, p < n_p - 1, combine, m - 1)]
         plan += back(m)
         if m + 1 < micros:
             plan += [step(late_dispatch, m + 1)]
             plan += both_of(tail(m), head(m + 1))
-    plan += tail(micros - 1) + [step(combine, micros - 1)]
+    plan += tail(micros - 1)
+    plan += [step(when, p == n_p - 1, combine, m) for m in range(micros - 1)]
+    plan += [step(combine, micros - 1)]
     for go in plan:
         go()
 

time: 111 us -> 99.3 us (0.89)
  Pallas kernels: 108 us -> 97.4 us
    pallas_call x1, Pallas kernels: 108 us -> 97.4 us  [local(): pl.pallas_call(functools.partial(layer_kernel, sizes), out_shape=jax.Shap...]
where the time goes in v2:
time: 99.3 us; the launch traced here: 99.1 us
  Pallas kernels  97.4 us (98%)
  local copies, waits for them, and re-layouts  1.67 us (2%)
    pallas_call x1, Pallas kernels, local(): pl.pallas_call(functools.partial(layer_kernel, sizes), out_shape=jax.Shap...  97.4 us

profile of v2, /device:TPU:2, one launch (start us, length us, event | category | flops | bytes accessed | tf_op | source)
XLA Modules:
  0.0 99.1 jit_solution(9430492776916441295)
XLA Ops:
  0.0 97.4 %shard_map.82 = bf16[1,2,64,1024]{3,2,1,0:T(8,128)(2,1)} custom-call(bf16[2,64,4096]{2,1,0:T(8,128)(2,1)} %tokens.1, f32[1,4096]{1,0:T(1,128)} %gains.1, s32[2,2,64]{2,1,0:T(2,128)} %bitcast.9, f32[2,2,64]{2,1,0:T(2,128)} %bitcast.10, s32[2,1,64]{2,1,0:T(1,128)} %bitcast.11, bf16[1,1,4096,384]{3,2,1,0:T(8,128)(2,1)} %w_gate.1, ...), custom_call_target="tpu_custom_call" | custom-call | tf_op jit(solution)/shard_map/pallas_call | solution.py:385
  97.4 1.7 %copy.11 = bf16[1,2,64,1024]{3,2,1,0:T(8,128)(2,1)} copy(bf16[1,2,64,1024]{3,2,1,0:T(8,128)(2,1)} %shard_map.82) | data formatting | bytes 524288

commit v3 on v2

--- a/solution.py
+++ b/solution.py
@@ -112,10 +112,13 @@
             found.append(jnp.where(kept, block * capacity + slot, -1))
         return found
 
-    def place(m):
+    def place(m, targets):
         places = lax.broadcasted_iota(jnp.int32, (rows_ge, toks), 0)
-        for e, target in enumerate(slots(m)):
+        for e, target in enumerate(targets):
             placing[m, e] = jnp.where(places == row_of(target), 1.0, 0.0).astype(BF16)
+
+    def weigh(m, targets):
+        for e, target in enumerate(targets):
             w_row = jnp.zeros((1, toks), F32)
             for k in range(ids.shape[1]):
                 w_row = w_row + jnp.where(ids[m, k:k + 1] == e, weights[m, k:k + 1], 0.0)
@@ -125,8 +128,7 @@
             comb[m, e, :toks] = high
             comb[m, e, toks:] = (w_col - high.astype(F32)).astype(BF16)
 
-    for m in range(micros):
-        place(m)
+    place(0, slots(0))
 
     ends = jnp.where(p > 0, 1, 0) + jnp.where(p < n_p - 1, 1, 0)
     pl.semaphore_wait(barrier, n_e - 1 + n_a - 1 + pair - 1 + ends)
@@ -244,8 +246,10 @@
                 if pair > 1:
                     total = total + p_recv[m, h, da, part].astype(F32)
                 y_send[m, d, da] = total.astype(BF16)
-                if da:
+                if da and d:
                     y_copy(m, d, da).start()
+            if h and da:
+                y_copy(m, 0, da).start()
 
     def reduce_far(m, d):
         total = y_send[m, d, 0].astype(F32)
@@ -259,7 +263,7 @@
             ret[m, z] = total.astype(BF16)
 
     def combine(m):
-        for d in range(n_e):
+        for d in halves[0] + halves[1]:
             e = peer_e(d)
             if d:
                 z_copy(m, d).wait_recv()
@@ -304,7 +308,7 @@
         return [step(compute, m, 1), step(reduce_pair, m, 1)]
 
     def tail(m):
-        return [step(reduce_far, m, d) for d in first[1:] + first[:1] + second]
+        return [step(reduce_far, m, d) for d in first[1:] + second + first[:1]]
 
     def both_of(one, two):
         mixed = []
@@ -313,18 +317,24 @@
         return mixed
 
     dispatch(0)
+    head(0)[0]()
+    for m in range(1, micros):
+        place(m, slots(m))
 
     @pl.when(p == 0)
     def _():
         for m in range(1, micros):
             dispatch(m)
 
+    for m in range(micros):
+        weigh(m, slots(m))
+
     def late_dispatch(m):
         @pl.when(p > 0)
         def _():
             dispatch(m)
 
-    plan = head(0)
+    plan = head(0)[1:]
     for m in range(micros):
         plan += middle(m)
         if m:

time: 99.3 us -> 101 us (1.017)
  no operation moved by 1% of the time
where the time goes in v3:
time: 101 us; the launch traced here: 99.8 us
  Pallas kernels  98.2 us (97%)
  local copies, waits for them, and re-layouts  1.67 us (2%)
    pallas_call x1, Pallas kernels, local(): pl.pallas_call(functools.partial(layer_kernel, sizes), out_shape=jax.Shap...  98.2 us

profile of v3, /device:TPU:2, one launch (start us, length us, event | category | flops | bytes accessed | tf_op | source)
XLA Modules:
  0.0 99.8 jit_solution(4373260182614846507)
XLA Ops:
  0.0 98.2 %shard_map.82 = bf16[1,2,64,1024]{3,2,1,0:T(8,128)(2,1)} custom-call(bf16[2,64,4096]{2,1,0:T(8,128)(2,1)} %tokens.1, f32[1,4096]{1,0:T(1,128)} %gains.1, s32[2,2,64]{2,1,0:T(2,128)} %bitcast.9, f32[2,2,64]{2,1,0:T(2,128)} %bitcast.10, s32[2,1,64]{2,1,0:T(1,128)} %bitcast.11, bf16[1,1,4096,384]{3,2,1,0:T(8,128)(2,1)} %w_gate.1, ...), custom_call_target="tpu_custom_call" | custom-call | tf_op jit(solution)/shard_map/pallas_call | solution.py:395
  98.2 1.7 %copy.11 = bf16[1,2,64,1024]{3,2,1,0:T(8,128)(2,1)} copy(bf16[1,2,64,1024]{3,2,1,0:T(8,128)(2,1)} %shard_map.82) | data formatting | bytes 524288

commit v4 on v3

--- a/solution.py
+++ b/solution.py
@@ -14,10 +14,10 @@
 
 
 def layer_kernel(
-    sizes, tokens, gains, ids, weights, picks, w_gate, w_up, w_down, out,
-    placing, comb, h_in, fresh, send, x, wg, wu, wd, g_acc, u_acc, own, p_send, p_recv,
+    sizes, tokens, gains_in, ids_in, weights_in, picks_in, w_gate, w_up, w_down, out,
+    gains, ids, weights, picks, placing, comb, h_in, fresh, send, x, wg, wu, wd, g_acc, u_acc, own, p_send, p_recv,
     y_send, y_recv, z_send, ret,
-    w_sem, h_loc, h_send, h_recv, d_send, d_recv, f_send, f_recv, c_send, c_recv,
+    s_sem, w_sem, h_loc, h_send, h_recv, d_send, d_recv, f_send, f_recv, c_send, c_recv,
     ps_sem, pr_sem, ys_sem, yr_sem, zs_sem, zr_sem,
 ):
     micros, n_p, n_t, n_e, pair, rows_ge, width, capacity = sizes
@@ -56,6 +56,15 @@
     def first_load(m):
         cols = pl.ds(pl.multiple_of(r * width, width), width)
         return pltpu.make_async_copy(tokens.at[m, :, cols], h_in.at[m], h_loc.at[m])
+
+    small = [
+        pltpu.make_async_copy(src, dst, s_sem.at[i])
+        for i, (src, dst) in enumerate(
+            [(picks_in, picks), (ids_in, ids), (weights_in, weights), (gains_in, gains)]
+        )
+    ]
+    for load in small:
+        load.start()
 
     @pl.when(p == 0)
     def _():
@@ -117,8 +126,8 @@
         for e, target in enumerate(targets):
             placing[m, e] = jnp.where(places == row_of(target), 1.0, 0.0).astype(BF16)
 
-    def weigh(m, targets):
-        for e, target in enumerate(targets):
+    def weigh(m):
+        for e, target in enumerate(slots(m)):
             w_row = jnp.zeros((1, toks), F32)
             for k in range(ids.shape[1]):
                 w_row = w_row + jnp.where(ids[m, k:k + 1] == e, weights[m, k:k + 1], 0.0)
@@ -128,6 +137,8 @@
             comb[m, e, :toks] = high
             comb[m, e, toks:] = (w_col - high.astype(F32)).astype(BF16)
 
+    for load in small:
+        load.wait()
     place(0, slots(0))
 
     ends = jnp.where(p > 0, 1, 0) + jnp.where(p < n_p - 1, 1, 0)
@@ -240,16 +251,14 @@
         for da in list(range(1, n_a)) + [0]:
             if pair > 1:
                 p_copy(m, h, da).wait_recv()
-            for i, d in enumerate(halves[h]):
+            for i, d in reversed(list(enumerate(halves[h]))) if h == 0 else enumerate(halves[h]):
                 part = slice(i * rows_ge, (i + 1) * rows_ge)
                 total = own[m, h, da, part].astype(F32)
                 if pair > 1:
                     total = total + p_recv[m, h, da, part].astype(F32)
                 y_send[m, d, da] = total.astype(BF16)
-                if da and d:
+                if da:
                     y_copy(m, d, da).start()
-            if h and da:
-                y_copy(m, 0, da).start()
 
     def reduce_far(m, d):
         total = y_send[m, d, 0].astype(F32)
@@ -301,14 +310,14 @@
         else:
             steps += [step(forward, m, d) for d in second[1:]]
         steps += [step(pass_on, m, d) for d in second[:-1]]
-        steps += [step(reduce_pair, m, 0), step(pass_on, m, second[-1])]
+        steps += [step(reduce_pair, m, 0), step(weigh, m), step(pass_on, m, second[-1])]
         return steps
 
     def back(m):
         return [step(compute, m, 1), step(reduce_pair, m, 1)]
 
     def tail(m):
-        return [step(reduce_far, m, d) for d in first[1:] + second + first[:1]]
+        return [step(reduce_far, m, d) for d in first[1:] + first[:1] + second]
 
     def both_of(one, two):
         mixed = []
@@ -325,9 +334,6 @@
     def _():
         for m in range(1, micros):
             dispatch(m)
-
-    for m in range(micros):
-        weigh(m, slots(m))
 
     def late_dispatch(m):
         @pl.when(p > 0)
@@ -391,13 +397,17 @@
     sizes = (micros, n_p, n_t, n_e, pair, rows_ge, width, capacity)
     dma = pltpu.SemaphoreType.DMA
     vmem = pl.BlockSpec(memory_space=pltpu.VMEM)
-    anywhere = pl.BlockSpec(memory_space=pl.ANY)
+    pinned = pl.BlockSpec(memory_space=pl.ANY)
     return pl.pallas_call(
         functools.partial(layer_kernel, sizes),
         out_shape=jax.ShapeDtypeStruct((1, micros, toks, width), BF16),
-        in_specs=[anywhere, vmem, vmem, vmem, vmem, anywhere, anywhere, anywhere],
+        in_specs=[pinned] * 8,
         out_specs=vmem,
         scratch_shapes=[
+            pltpu.VMEM(gains.shape, F32),
+            pltpu.VMEM(ids.shape, jnp.int32),
+            pltpu.VMEM(weights.shape, F32),
+            pltpu.VMEM(order.shape, jnp.int32),
             pltpu.VMEM((micros, n_e, rows_ge, toks), BF16),
             pltpu.VMEM((micros, n_e, 2 * toks, rows_ge), BF16),
             pltpu.VMEM((micros, toks, width), BF16),
@@ -416,7 +426,7 @@
             pltpu.VMEM((micros, n_e, n_a, rows_ge, width), BF16),
             pltpu.VMEM((micros, n_e, rows_ge, width), BF16),
             pltpu.VMEM((micros, n_e, rows_ge, width), BF16),
-            dma((3,)), dma((micros,)), dma((micros,)), dma((micros,)),
+            dma((4,)), dma((3,)), dma((micros,)), dma((micros,)), dma((micros,)),
             dma((micros, n_e)), dma((micros, n_e)),
             dma((micros, n_e, n_a)), dma((micros, n_e, n_a)),
             dma((micros, n_e, n_a)), dma((micros, n_e, n_a)),
@@ -425,7 +435,7 @@
             dma((micros, n_e)), dma((micros, n_e)),
         ],
         compiler_params=pltpu.CompilerParams(
-            collective_id=0, has_side_effects=True, vmem_limit_bytes=67043328 - 600 * 1024
+            collective_id=0, has_side_effects=True, vmem_limit_bytes=67043328
         ),
     )(tokens, gains, ids, weights, order, w_gate, w_up, w_down)
 

time: 101 us -> 98.7 us (0.977)
  Pallas kernels: 98.2 us -> 96.7 us
    pallas_call x1, Pallas kernels: 98.2 us -> 96.7 us  [local(): pl.pallas_call(functools.partial(layer_kernel, sizes), out_shape=jax.Shap...]
where the time goes in v4:
time: 98.7 us; the launch traced here: 98.4 us
  Pallas kernels  96.7 us (98%)
  local copies, waits for them, and re-layouts  1.67 us (2%)
    pallas_call x1, Pallas kernels, local(): pl.pallas_call(functools.partial(layer_kernel, sizes), out_shape=jax.Shap...  96.7 us

profile of v4, /device:TPU:2, one launch (start us, length us, event | category | flops | bytes accessed | tf_op | source)
XLA Modules:
  0.0 98.4 jit_solution(1438080304672328747)
XLA Ops:
  0.0 96.7 %shard_map.82 = bf16[1,2,64,1024]{3,2,1,0:T(8,128)(2,1)} custom-call(bf16[2,64,4096]{2,1,0:T(8,128)(2,1)} %tokens.1, f32[1,4096]{1,0:T(1,128)} %gains_in.1, s32[2,2,64]{2,1,0:T(2,128)} %bitcast.9, f32[2,2,64]{2,1,0:T(2,128)} %bitcast.10, s32[2,1,64]{2,1,0:T(1,128)} %bitcast.11, bf16[1,1,4096,384]{3,2,1,0:T(8,128)(2,1)} %w_gate.1, ...), custom_call_target="tpu_custom_call" | custom-call | tf_op jit(solution)/shard_map/pallas_call | solution.py:401
  96.7 1.7 %copy.11 = bf16[1,2,64,1024]{3,2,1,0:T(8,128)(2,1)} copy(bf16[1,2,64,1024]{3,2,1,0:T(8,128)(2,1)} %shard_map.82) | data formatting | bytes 524288
